TPU v7x, 32 devices: a whole 2x2x4 slice. The times are simulated.
32 devices in a mesh: row: 4 (over y, x), col: 8 (over z, core).
Axes of the slice: x: 2, y: 2, z: 4, core: 2. Of those that a mesh axis runs over, the one named last changes fastest.
Arguments:
- initial_field: float32 [256, 256, 256], P(('row', 'col')), may hold values from -5 to 5
Outputs:
- advanced_field: float32 [256, 256, 256], P(('row', 'col'))
All inputs are finite; a program needn't handle non-finite values.
Results may differ from a plain program's by a relative error of at most 0.0003.
Values sent between devices are 32-bit elements; how exact they have to be, the bound alone decides.
A program may use at most 128 MiB of HBM per device.

v0:
```python
import functools
import math

import jax
import jax.numpy as jnp
import numpy as np
from jax import lax
from jax.experimental import pallas as pl
from jax.experimental.pallas import tpu as pltpu
from jax.sharding import PartitionSpec as P

growth_rate = 0.3
quadratic = 1.0
time_step = 0.2
wave_scale = 4.0


def wavenumbers(count, offset, length):
    indices = offset + jnp.arange(count)
    signed = jnp.where(indices * 2 < length, indices, indices - length)
    return wave_scale * signed.astype(jnp.float32) / length


def phi_values(argument):
    within = jnp.abs(argument) < 1.0
    inside = jnp.where(within, argument, 0.0)
    outside = jnp.where(within, 2.0, argument)
    series = []
    for degree in (1, 2, 3):
        running = jnp.zeros_like(argument) + 1.0 / math.factorial(11 + degree)
        for exponent in range(10, -1, -1):
            running = running * inside + 1.0 / math.factorial(exponent + degree)
        series.append(running)
    growth_term = jnp.exp(outside)
    closed_one = (growth_term - 1.0) / outside
    closed_two = (growth_term - 1.0 - outside) / (outside * outside)
    closed_three = (growth_term - 1.0 - outside - 0.5 * outside * outside) / (
        outside * outside * outside
    )
    return (
        jnp.where(within, series[0], closed_one),
        jnp.where(within, series[1], closed_two),
        jnp.where(within, series[2], closed_three),
    )


def step_factors(ksq):
    lin = growth_rate - (1.0 - ksq) * (1.0 - ksq)
    scaled = time_step * lin
    half_phi, _, _ = phi_values(0.5 * scaled)
    first_phi, second_phi, third_phi = phi_values(scaled)
    e_half = jnp.exp(0.5 * scaled)
    q_half = 0.5 * time_step * half_phi
    e_full = jnp.exp(scaled)
    f_one = time_step * (first_phi - 3.0 * second_phi + 4.0 * third_phi)
    f_two = time_step * (second_phi - 2.0 * third_phi)
    f_three = time_step * (4.0 * third_phi - second_phi)
    return (e_half, q_half, e_full, f_one, f_two, f_three)


def reaction(values):
    return quadratic * values * values - values * values * values


def cas_table(length):
    modes = jnp.arange(length, dtype=jnp.int32)
    product = jnp.mod(modes[:, None] * modes[None, :], length)
    angle = 2.0 * math.pi / length * product.astype(jnp.float32)
    return (jnp.cos(angle) + jnp.sin(angle)) / math.sqrt(length)


def contract(form, left, right):
    return jnp.einsum(
        form, left, right, precision=lax.Precision.HIGHEST, preferred_element_type=jnp.float32
    )


def move(blocks):
    return lax.all_to_all(blocks, ("row", "col"), split_axis=0, concat_axis=0, tiled=True)


def plain_body(initial_field):
    devices_all = lax.axis_size("row") * lax.axis_size("col")
    rows_x, size_y, size_z = initial_field.shape
    size_x = rows_x * devices_all
    share_y = size_y // devices_all
    table_z = cas_table(size_z)
    table_y = cas_table(size_y).reshape((devices_all, share_y, size_y))
    table_x = cas_table(size_x).reshape((devices_all, rows_x, size_x))
    offset = lax.axis_index(("row", "col")) * share_y
    wave_y = wavenumbers(share_y, offset, size_y)
    wave_z = wavenumbers(size_z, 0, size_z)
    wave_x = wavenumbers(size_x, 0, size_x)
    ksq = wave_y[:, None, None] ** 2 + wave_z[None, None, :] ** 2 + wave_x[None, :, None] ** 2
    e_half, q_half, e_full, f_one, f_two, f_three = step_factors(ksq)

    def forward_all(values):
        over_z = contract("xyn,nk->xyk", values, table_z)
        over_y = contract("sly,xyk->slxk", table_y, over_z)
        return contract("sxX,slxk->lXk", table_x, move(over_y))

    def inverse_all(spectra):
        over_x = contract("sxX,lXk->slxk", table_x, spectra)
        over_y = contract("slxk,sly->xyk", move(over_x), table_y)
        return contract("xyk,kn->xyn", over_y, table_z)

    def react_spectrum(spectrum):
        return forward_all(reaction(inverse_all(spectrum)))

    state_hat = forward_all(initial_field)
    react_u = forward_all(reaction(initial_field))
    first_hat = e_half * state_hat + q_half * react_u
    react_a = react_spectrum(first_hat)
    second_hat = e_half * state_hat + q_half * react_a
    react_b = react_spectrum(second_hat)
    third_hat = e_half * first_hat + q_half * (2.0 * react_b - react_u)
    react_c = react_spectrum(third_hat)
    new_hat = (
        e_full * state_hat + f_one * react_u + 2.0 * f_two * (react_a + react_b) + f_three * react_c
    )
    return inverse_all(new_hat)


LANES = 128


def split_table(length):
    modes = np.arange(length)
    angle = 2.0 * np.pi / length * ((modes[:, None] * modes[None, :]) % length)
    table = ((np.cos(angle) + np.sin(angle)) / np.sqrt(length)).astype(np.float32)
    upper = table.astype(jnp.bfloat16)
    lower = (table - upper.astype(np.float32)).astype(jnp.bfloat16)
    return upper, lower


def split_values(values):
    upper = values.astype(jnp.bfloat16)
    lower = (values - upper.astype(jnp.float32)).astype(jnp.bfloat16)
    return upper, lower


def kernel(
    count, columns, rows_x, share_y, size_x, size_y, size_z,
    field_in, left, right, out_to,
    send_f, got_f, send_i, got_i, held, third, total,
    e_half, q_half, e_full, f_one, f_two, f_three,
    sent_f, came_f, sent_i, came_i, field, out, plane_in, plane_out,
):
    me = lax.axis_index("row") * columns + lax.axis_index("col")
    block = rows_x * share_y
    halves = size_z // LANES
    pairs = share_y // 2
    group = 1
    parts = rows_x // group
    early = parts // 2

    def mul_left(values):
        upper, lower = split_values(values)
        stacked = jnp.concatenate([upper, lower, upper], axis=0)
        return jnp.dot(left[...], stacked, preferred_element_type=jnp.float32)

    def mul_right(values):
        upper, lower = split_values(values)
        stacked = jnp.concatenate([upper, lower, upper], axis=1)
        return jnp.dot(stacked, right[...], preferred_element_type=jnp.float32)

    def load(m):
        return pltpu.make_async_copy(field_in.at[m], field.at[m], plane_in.at[m])

    def store(m):
        return pltpu.make_async_copy(out.at[m], out_to.at[m], plane_out.at[m])

    for m in range(rows_x):
        load(m).start()
    barrier = pltpu.get_barrier_semaphore()

    def greet(offset, carry):
        other = (me + offset) % count
        pl.semaphore_signal(
            barrier,
            inc=1,
            device_id=(other // columns, other % columns),
            device_id_type=pl.DeviceIdType.MESH,
        )
        return carry

    lax.fori_loop(1, count, greet, 0)

    def send_forward(index, half, start, length):
        buffer = index % 2
        here = pl.multiple_of(me * block + start, 8)
        mine = got_f.at[buffer, half, pl.ds(here, length), :]
        pltpu.make_async_copy(
            send_f.at[buffer, half, me, pl.ds(start, length), :], mine, came_f.at[index, half]
        ).start()

        def one(offset, carry):
            other = (me + offset) % count
            pltpu.make_async_remote_copy(
                src_ref=send_f.at[buffer, half, other, pl.ds(start, length), :],
                dst_ref=mine,
                send_sem=sent_f.at[index, half],
                recv_sem=came_f.at[index, half],
                device_id=(other // columns, other % columns),
                device_id_type=pl.DeviceIdType.MESH,
            ).start()
            return carry

        lax.fori_loop(1, count, one, 0)

    def send_inverse(index, half, part):
        length = group * share_y
        mine = got_i.at[half, me, pl.ds(part * length, length), :]

        def rows(device):
            start = pl.multiple_of(device * block + part * length, 8)
            return send_i.at[half, pl.ds(start, length), :]

        pltpu.make_async_copy(rows(me), mine, came_i.at[index, part]).start()

        def one(offset, carry):
            other = (me + offset) % count
            pltpu.make_async_remote_copy(
                src_ref=rows(other),
                dst_ref=mine,
                send_sem=sent_i.at[index, half],
                recv_sem=came_i.at[index, part],
                device_id=(other // columns, other % columns),
                device_id_type=pl.DeviceIdType.MESH,
            ).start()
            return carry

        lax.fori_loop(1, count, one, 0)

    def wait_bytes(ref, sem):
        pltpu.make_async_copy(ref, ref, sem).wait()

    def wait_sent_forward(index):
        for half in range(halves):
            wait_bytes(send_f.at[index % 2, half, pl.ds(0, count - 1)], sent_f.at[index, half])

    def wait_sent_inverse(index, half):
        wait_bytes(send_i.at[half, pl.ds(0, (count - 1) * block), :], sent_i.at[index, half])

    def forward(index, source, before=None):
        def plane(m):
            spectrum = mul_left(mul_right(source(m)))
            rows = pl.ds(pl.multiple_of(m * share_y, 8), share_y)
            for half in range(halves):
                part = spectrum[:, half * LANES : (half + 1) * LANES]
                send_f[index % 2, half, :, rows, :] = part.reshape(count, share_y, LANES)

        def step(g, carry):
            if before is not None:
                before(g)
            for inner in range(group):
                plane(g * group + inner)
            send_forward(
                index, 0, pl.multiple_of(g * group * share_y, 8), group * share_y
            )
            return carry

        first = 0
        if index == 0:
            for m in range(group):
                load(m).wait()
                plane(m)
            pl.semaphore_wait(barrier, count - 1)
            send_forward(0, 0, 0, group * share_y)
            first = 1
        lax.fori_loop(first, parts, step, 0)
        for half in range(1, halves):
            send_forward(index, half, 0, block)

    def physical(m):
        rows = pl.ds(pl.multiple_of(m * share_y, 8), share_y)
        parts = [got_i[half, :, rows, :].reshape(size_y, LANES) for half in range(halves)]
        return mul_right(mul_left(jnp.concatenate(parts, axis=1)))

    def spectrum_at(index, half, pair):
        parts = [
            got_f[index % 2, half, pl.ds(pair * 2 + inner, size_x, stride=share_y), :]
            for inner in range(2)
        ]
        return mul_left(jnp.concatenate(parts, axis=1))

    def arrived_forward(index, half):
        wait_bytes(got_f.at[index % 2, half], came_f.at[index, half])

    def inverse(index, source, update):
        for half in range(halves):
            arrived_forward(source, half)
            if index > 0:
                wait_sent_inverse(index - 1, half)

            def step(pair, carry):
                values = mul_left(update(half, pair, spectrum_at(source, half, pair)))
                for inner in range(2):
                    send_i[half, pl.ds(pair * 2 + inner, size_x, stride=share_y), :] = values[
                        :, inner * LANES : (inner + 1) * LANES
                    ]
                return carry

            lax.fori_loop(0, pairs, step, 0)
            for part in range(early):
                send_inverse(index, half, part)
        for part in range(early, parts):
            for half in range(halves):
                send_inverse(index, half, part)

    def arrived_inverse(index, part):
        length = group * share_y
        rows = pl.ds(pl.multiple_of(part * length, 8), length)
        wait_bytes(got_i.at[:, :, rows, :], came_i.at[index, part])

    def wave(indices, length):
        signed = jnp.where(indices * 2 < length, indices, indices - length)
        return wave_scale * signed.astype(jnp.float32) / length

    def loaded(g):
        for inner in range(group):
            load(g * group + inner).wait()

    forward(0, lambda m: field[m], loaded)
    forward(1, lambda m: reaction(field[m]))

    rows_step = 32

    def factors(item, carry):
        half = item // (pairs * (size_x // rows_step))
        rest = item % (pairs * (size_x // rows_step))
        pair = rest // (size_x // rows_step)
        start = pl.multiple_of(rest % (size_x // rows_step) * rows_step, 8)
        dims = (rows_step, 2 * LANES)
        lane = lax.broadcasted_iota(jnp.int32, dims, 1)
        second = (lane >= LANES).astype(jnp.int32)
        index_z = lane - second * LANES + half * LANES
        index_y = second + (me * share_y + pair * 2)
        index_x = lax.broadcasted_iota(jnp.int32, dims, 0) + start
        wave_y, wave_z, wave_x = wave(index_y, size_y), wave(index_z, size_z), wave(index_x, size_x)
        ksq = wave_y * wave_y + wave_z * wave_z + wave_x * wave_x
        values = step_factors(ksq)
        where = pl.ds(start, rows_step)
        for ref, value in zip((e_half, q_half, e_full, f_one, f_two, f_three), values):
            ref[half, pair, where, :] = value
        return carry

    lax.fori_loop(0, halves * pairs * (size_x // rows_step), factors, 0)

    for half in range(halves):
        arrived_forward(0, half)

        def keep(pair, carry):
            total[half, pair] = spectrum_at(0, half, pair)
            return carry

        lax.fori_loop(0, pairs, keep, 0)

    def update_first(half, pair, react_u):
        state_hat = total[half, pair]
        base = e_half[half, pair] * state_hat
        gain = q_half[half, pair] * react_u
        first_hat = base + gain
        held[half, pair] = base
        third[half, pair] = e_half[half, pair] * first_hat - gain
        total[half, pair] = e_full[half, pair] * state_hat + f_one[half, pair] * react_u
        return first_hat

    def update_second(half, pair, react_a):
        total[half, pair] = total[half, pair] + 2.0 * f_two[half, pair] * react_a
        return held[half, pair] + q_half[half, pair] * react_a

    def update_third(half, pair, react_b):
        total[half, pair] = total[half, pair] + 2.0 * f_two[half, pair] * react_b
        return third[half, pair] + 2.0 * q_half[half, pair] * react_b

    def update_last(half, pair, react_c):
        return total[half, pair] + f_three[half, pair] * react_c

    updates = (update_first, update_second, update_third, update_last)
    for index, update in enumerate(updates):
        inverse(index, index + 1, update)
        if index < 3:
            wait_sent_forward(index)
            forward(
                index + 2,
                lambda m: reaction(physical(m)),
                lambda g, index=index: arrived_inverse(index, g),
            )
    for index in (3, 4):
        wait_sent_forward(index)

    def finish(g, carry):
        arrived_inverse(3, g)
        for inner in range(group):
            out[g * group + inner] = physical(g * group + inner)
            store(g * group + inner).start()
        return carry

    lax.fori_loop(0, parts, finish, 0)
    for half in range(halves):
        wait_sent_inverse(3, half)
    for m in range(rows_x):
        store(m).wait()


def body(initial_field):
    rows_x, size_y, size_z = initial_field.shape
    columns = lax.axis_size("col")
    count = lax.axis_size("row") * columns
    size_x = rows_x * count
    share_y = size_y // count
    fits = share_y % 8 == 0 and size_z % LANES == 0 and size_x == size_y == size_z
    if not fits:
        return plain_body(initial_field)
    upper, lower = split_table(size_x)
    left = np.concatenate([upper, upper, lower], axis=1)
    right = np.concatenate([upper, upper, lower], axis=0)
    halves, pairs, block = size_z // LANES, share_y // 2, rows_x * share_y
    spectral = pltpu.VMEM((halves, pairs, size_x, 2 * LANES), jnp.float32)
    vmem = pl.BlockSpec(memory_space=pltpu.VMEM)
    return pl.pallas_call(
        functools.partial(
            kernel, count, columns, rows_x, share_y, size_x, size_y, size_z
        ),
        out_shape=jax.ShapeDtypeStruct(initial_field.shape, jnp.float32),
        in_specs=[pl.BlockSpec(memory_space=pltpu.HBM), vmem, vmem],
        out_specs=pl.BlockSpec(memory_space=pltpu.HBM),
        scratch_shapes=[
            pltpu.VMEM((2, halves, count, block, LANES), jnp.float32),
            pltpu.VMEM((2, halves, count * block, LANES), jnp.float32),
            pltpu.VMEM((halves, count * block, LANES), jnp.float32),
            pltpu.VMEM((halves, count, block, LANES), jnp.float32),
        ]
        + [spectral] * 9
        + [
            pltpu.SemaphoreType.DMA((5, halves)),
            pltpu.SemaphoreType.DMA((5, halves)),
            pltpu.SemaphoreType.DMA((4, halves)),
            pltpu.SemaphoreType.DMA((4, rows_x)),
            pltpu.VMEM(initial_field.shape, jnp.float32),
            pltpu.VMEM(initial_field.shape, jnp.float32),
            pltpu.SemaphoreType.DMA((rows_x,)),
            pltpu.SemaphoreType.DMA((rows_x,)),
        ],
        compiler_params=pltpu.CompilerParams(
            collective_id=0, has_side_effects=True, vmem_limit_bytes=60 * 1024 * 1024
        ),
    )(initial_field, jnp.asarray(left), jnp.asarray(right))


def solution(mesh):
    placed = (P(("row", "col"), None, None),)
    return jax.shard_map(
        body, mesh=mesh, in_specs=placed, out_specs=P(("row", "col"), None, None), check_vma=False
    )
```

profile of v0, /device:TPU:0, one launch (start us, length us, event | category | flops | bytes accessed | tf_op | source)
XLA Modules:
  0.0 419.3 jit_solution(929879968711143295)
XLA Ops:
  0.0 416.2 %shard_map.37 = f32[8,256,256]{2,1,0:T(8,128)} custom-call(f32[8,256,256]{2,1,0:T(8,128)} %field_in.1, bf16[256,768]{1,0:T(8,128)(2,1)} %constant.4.clone.left, bf16[768,256]{1,0:T(8,128)(2,1)} %constant.5.clone.right), custom_call_target="tpu_custom_call" | custom-call | tf_op jit(solution)/shard_map/pallas_call | solution.py:422
  416.2 3.0 copy.5
where the time goes:
time: 419 us
  Pallas kernels  416 us (99%)
    pallas_call x1, Pallas kernels, body(): pl.pallas_call(functools.partial(kernel, count, columns, rows_x, share_y,...  416 us

commit v1 on v0

v1 whole, which is shorter than its diff:
```python
import functools
import math

import jax
import jax.numpy as jnp
import numpy as np
from jax import lax
from jax.experimental import pallas as pl
from jax.experimental.pallas import tpu as pltpu
from jax.sharding import PartitionSpec as P

growth_rate = 0.3
quadratic = 1.0
time_step = 0.2
wave_scale = 4.0


def wavenumbers(count, offset, length):
    indices = offset + jnp.arange(count)
    signed = jnp.where(indices * 2 < length, indices, indices - length)
    return wave_scale * signed.astype(jnp.float32) / length


def phi_values(argument):
    within = jnp.abs(argument) < 1.0
    inside = jnp.where(within, argument, 0.0)
    outside = jnp.where(within, 2.0, argument)
    series = []
    for degree in (1, 2, 3):
        running = jnp.zeros_like(argument) + 1.0 / math.factorial(11 + degree)
        for exponent in range(10, -1, -1):
            running = running * inside + 1.0 / math.factorial(exponent + degree)
        series.append(running)
    growth_term = jnp.exp(outside)
    closed_one = (growth_term - 1.0) / outside
    closed_two = (growth_term - 1.0 - outside) / (outside * outside)
    closed_three = (growth_term - 1.0 - outside - 0.5 * outside * outside) / (
        outside * outside * outside
    )
    return (
        jnp.where(within, series[0], closed_one),
        jnp.where(within, series[1], closed_two),
        jnp.where(within, series[2], closed_three),
    )


def step_factors(ksq):
    lin = growth_rate - (1.0 - ksq) * (1.0 - ksq)
    scaled = time_step * lin
    half_phi, _, _ = phi_values(0.5 * scaled)
    first_phi, second_phi, third_phi = phi_values(scaled)
    e_half = jnp.exp(0.5 * scaled)
    q_half = 0.5 * time_step * half_phi
    e_full = jnp.exp(scaled)
    f_one = time_step * (first_phi - 3.0 * second_phi + 4.0 * third_phi)
    f_two = time_step * (second_phi - 2.0 * third_phi)
    f_three = time_step * (4.0 * third_phi - second_phi)
    return (e_half, q_half, e_full, f_one, f_two, f_three)


def reaction(values):
    return quadratic * values * values - values * values * values


def cas_table(length):
    modes = jnp.arange(length, dtype=jnp.int32)
    product = jnp.mod(modes[:, None] * modes[None, :], length)
    angle = 2.0 * math.pi / length * product.astype(jnp.float32)
    return (jnp.cos(angle) + jnp.sin(angle)) / math.sqrt(length)


def contract(form, left, right):
    return jnp.einsum(
        form, left, right, precision=lax.Precision.HIGHEST, preferred_element_type=jnp.float32
    )


def move(blocks):
    return lax.all_to_all(blocks, ("row", "col"), split_axis=0, concat_axis=0, tiled=True)


def plain_body(initial_field):
    devices_all = lax.axis_size("row") * lax.axis_size("col")
    rows_x, size_y, size_z = initial_field.shape
    size_x = rows_x * devices_all
    share_y = size_y // devices_all
    table_z = cas_table(size_z)
    table_y = cas_table(size_y).reshape((devices_all, share_y, size_y))
    table_x = cas_table(size_x).reshape((devices_all, rows_x, size_x))
    offset = lax.axis_index(("row", "col")) * share_y
    wave_y = wavenumbers(share_y, offset, size_y)
    wave_z = wavenumbers(size_z, 0, size_z)
    wave_x = wavenumbers(size_x, 0, size_x)
    ksq = wave_y[:, None, None] ** 2 + wave_z[None, None, :] ** 2 + wave_x[None, :, None] ** 2
    e_half, q_half, e_full, f_one, f_two, f_three = step_factors(ksq)

    def forward_all(values):
        over_z = contract("xyn,nk->xyk", values, table_z)
        over_y = contract("sly,xyk->slxk", table_y, over_z)
        return contract("sxX,slxk->lXk", table_x, move(over_y))

    def inverse_all(spectra):
        over_x = contract("sxX,lXk->slxk", table_x, spectra)
        over_y = contract("slxk,sly->xyk", move(over_x), table_y)
        return contract("xyk,kn->xyn", over_y, table_z)

    def react_spectrum(spectrum):
        return forward_all(reaction(inverse_all(spectrum)))

    state_hat = forward_all(initial_field)
    react_u = forward_all(reaction(initial_field))
    first_hat = e_half * state_hat + q_half * react_u
    react_a = react_spectrum(first_hat)
    second_hat = e_half * state_hat + q_half * react_a
    react_b = react_spectrum(second_hat)
    third_hat = e_half * first_hat + q_half * (2.0 * react_b - react_u)
    react_c = react_spectrum(third_hat)
    new_hat = (
        e_full * state_hat + f_one * react_u + 2.0 * f_two * (react_a + react_b) + f_three * react_c
    )
    return inverse_all(new_hat)


LANES = 128
CORES = 2
LAYERS = 4
ROWS = 8


def split_table(length):
    modes = np.arange(length)
    angle = 2.0 * np.pi / length * ((modes[:, None] * modes[None, :]) % length)
    table = ((np.cos(angle) + np.sin(angle)) / np.sqrt(length)).astype(np.float32)
    upper = table.astype(jnp.bfloat16)
    lower = (table - upper.astype(np.float32)).astype(jnp.bfloat16)
    return upper, lower


def split_values(values):
    upper = values.astype(jnp.bfloat16)
    lower = (values - upper.astype(jnp.float32)).astype(jnp.bfloat16)
    return upper, lower


def kernel(
    count, columns, rows_x, share_y, size_x, size_y, size_z,
    field_in, left, right, out_to,
    send_f, got_f, send_i, got_i, held, third, total, q_half, f_two, f_three, field,
    came_f, twin_f, sent_f, passed_f, came_i, near_i, twin_i, sent_i, passed_i,
    swapped, swap_sent, plane_in, plane_out,
):
    row, col = lax.axis_index("row"), lax.axis_index("col")
    me = row * columns + col
    layer, core = col // CORES, col % CORES
    groups = count // LAYERS
    my_group = row * CORES + core
    middle = jnp.logical_and(layer > 0, layer < LAYERS - 1)
    units = jnp.where(middle, 2, 1)
    home = jnp.where(middle, layer - 1, 0)
    outer = jnp.where(layer < LAYERS // 2, 0, LAYERS - 1)
    near = jnp.where(layer < LAYERS // 2, 1, LAYERS - 2)
    twin = row * columns + (LAYERS - 1 - layer) * CORES + core
    block = rows_x * share_y
    halves = size_z // LANES
    pairs = share_y // 2
    parts = rows_x
    early = parts // 2
    chunks = 4
    chunk = block // chunks
    e_half = third

    def target(device):
        return dict(
            device_id=(device // columns, device % columns), device_id_type=pl.DeviceIdType.MESH
        )

    def unit_at(slot):
        return row * columns + jnp.where(middle, slot + 1, layer) * CORES + core

    def mul_left(values):
        upper, lower = split_values(values)
        stacked = jnp.concatenate([upper, lower, upper], axis=0)
        return jnp.dot(left[...], stacked, preferred_element_type=jnp.float32)

    def mul_right(values):
        upper, lower = split_values(values)
        stacked = jnp.concatenate([upper, lower, upper], axis=1)
        return jnp.dot(stacked, right[...], preferred_element_type=jnp.float32)

    def load(m):
        return pltpu.make_async_copy(field_in.at[m], field.at[home, m], plane_in.at[m])

    def store(m):
        return pltpu.make_async_copy(field.at[0, m], out_to.at[m], plane_out.at[m])

    def swap(m):
        return pltpu.make_async_remote_copy(
            src_ref=field_in.at[m],
            dst_ref=field.at[home, m],
            send_sem=swap_sent,
            recv_sem=swapped.at[m],
            **target(twin),
        )

    def wait_bytes(ref, sem):
        pltpu.make_async_copy(ref, ref, sem).wait()

    def send_forward(index, half, slot, start, length, near_sem):
        buffer = index % 2
        source_rows = pl.ds(pl.multiple_of(slot * block + start, 8), length)
        target_rows = pl.ds(pl.multiple_of(unit_at(slot) * block + start, 8), length)
        sent, came = sent_f.at[index, half], came_f.at[index, half]

        def single(group, to):
            return dict(
                src_ref=send_f.at[buffer, half, group // CORES, to, group % CORES, source_rows, :],
                dst_ref=got_f.at[buffer, half, 0, target_rows, :],
            )

        def double(group):
            return dict(
                src_ref=send_f.at[
                    buffer, half, group // CORES, pl.ds(1, 2), group % CORES, source_rows, :
                ],
                dst_ref=got_f.at[buffer, half, :, target_rows, :],
            )

        def away(refs, group, to, sem):
            device = (group // CORES) * columns + to * CORES + group % CORES
            pltpu.make_async_remote_copy(
                **refs, send_sem=sent, recv_sem=sem, **target(device)
            ).start()

        def own(refs):
            pltpu.make_async_copy(refs["src_ref"], refs["dst_ref"], came).start()

        @pl.when(middle)
        def _():
            own(double(my_group))
            away(single(my_group, outer), my_group, outer, came)

            def one(offset, carry):
                group = (my_group + offset) % groups
                away(single(group, outer), group, outer, came)
                away(double(group), group, layer, came)
                return carry

            lax.fori_loop(1, groups, one, 0)

        @pl.when(jnp.logical_not(middle))
        def _():
            own(single(my_group, layer))

            def one(offset, carry):
                group = (my_group + offset) % groups
                away(double(group), group, near, came_f.at[index, near_sem])
                away(single(group, LAYERS - 1 - layer), group, LAYERS - 1 - layer, came)

                @pl.when(offset > 0)
                def _():
                    away(single(group, layer), group, layer, came)

                return carry

            lax.fori_loop(0, groups, one, 0)

    def pass_forward(index, half, start, length, near_sem):
        buffer = index % 2

        @pl.when(middle)
        def _():
            wait_bytes(
                got_f.at[buffer, half, :, pl.ds(0, groups * length), :],
                came_f.at[index, near_sem],
            )

            def one(group, carry):
                unit = (group // CORES) * columns + outer * CORES + group % CORES
                region = got_f.at[
                    buffer, half, :, pl.ds(pl.multiple_of(unit * block + start, 8), length), :
                ]
                pltpu.make_async_remote_copy(
                    src_ref=region,
                    dst_ref=region,
                    send_sem=passed_f.at[index],
                    recv_sem=twin_f.at[index, half],
                    **target(twin),
                ).start()
                return carry

            lax.fori_loop(0, groups, one, 0)

    def pass_forward_part(index, part):
        pass_forward(index, 0, part * share_y, share_y, 2 + part)

    def pass_forward_chunk(index, number):
        pass_forward(index, 1, number * chunk, chunk, 2 + parts + number)

    def send_second_half(index):
        def slot_loop(slot, carry):
            def one(number, inner):
                send_forward(index, 1, slot, number * chunk, chunk, 2 + parts + number)
                return inner

            return lax.fori_loop(0, chunks, one, carry)

        lax.fori_loop(0, units, slot_loop, 0)

    def send_inverse(index, half, part):
        start = part * share_y
        sent, came = sent_i.at[index, half], came_i.at[index, part]
        mine = pl.ds(pl.multiple_of(start, 8), share_y)

        def rows_of(group, to):
            unit = (group // CORES) * columns + to * CORES + group % CORES
            return pl.ds(pl.multiple_of(unit * block + start, 8), share_y)

        def away(refs, group, to, sem):
            device = (group // CORES) * columns + to * CORES + group % CORES
            pltpu.make_async_remote_copy(
                **refs, send_sem=sent, recv_sem=sem, **target(device)
            ).start()

        def own(refs):
            pltpu.make_async_copy(refs["src_ref"], refs["dst_ref"], came).start()

        @pl.when(middle)
        def _():
            def refs(group, to, slot):
                return dict(
                    src_ref=send_i.at[half, :, rows_of(group, to), :],
                    dst_ref=got_i.at[slot, half, row, pl.ds(1, 2), core, mine, :],
                )

            for slot in range(2):
                own(refs(my_group, slot + 1, slot))
            away(refs(my_group, outer, 0), my_group, outer, came)

            def one(offset, carry):
                group = (my_group + offset) % groups
                away(refs(group, outer, 0), group, outer, came)
                for slot in range(2):
                    away(refs(group, slot + 1, slot), group, layer, came)
                return carry

            lax.fori_loop(1, groups, one, 0)

        @pl.when(jnp.logical_not(middle))
        def _():
            def refs(group, to, slot):
                return dict(
                    src_ref=send_i.at[half, 0, rows_of(group, to), :],
                    dst_ref=got_i.at[slot, half, row, layer, core, mine, :],
                )

            own(refs(my_group, layer, 0))

            def one(offset, carry):
                group = (my_group + offset) % groups
                for slot in range(2):
                    away(refs(group, slot + 1, slot), group, near, near_i.at[index, half, part])
                away(
                    refs(group, LAYERS - 1 - layer, 0), group, LAYERS - 1 - layer, came
                )

                @pl.when(offset > 0)
                def _():
                    away(refs(group, layer, 0), group, layer, came)

                return carry

            lax.fori_loop(0, groups, one, 0)

    def pass_inverse(index, half, part):
        mine = pl.ds(pl.multiple_of(part * share_y, 8), share_y)

        @pl.when(middle)
        def _():
            wait_bytes(got_i.at[:, half, :, 1, :, mine, :], near_i.at[index, half, part])

            def one(group, carry):
                region = got_i.at[:, half, group // CORES, outer, group % CORES, mine, :]
                pltpu.make_async_remote_copy(
                    src_ref=region,
                    dst_ref=region,
                    send_sem=passed_i.at[index],
                    recv_sem=twin_i.at[index, part],
                    **target(twin),
                ).start()
                return carry

            lax.fori_loop(0, groups, one, 0)

    def wait_sent(sem):
        @pl.when(middle)
        def _():
            wait_bytes(got_f.at[0, 0, :, pl.ds(0, (groups * 3 - 2) * block), :], sem)

        @pl.when(jnp.logical_not(middle))
        def _():
            wait_bytes(got_f.at[0, 0, 0, pl.ds(0, (groups * 4 - 1) * block), :], sem)

    def wait_sent_forward(index):
        for half in range(halves):
            wait_sent(sent_f.at[index, half])

    def wait_passed(sem):
        @pl.when(middle)
        def _():
            wait_bytes(got_f.at[0, 0, 0], sem)

    def plane(index, slot, m, values):
        spectrum = mul_left(mul_right(values))
        rows = pl.ds(pl.multiple_of(slot * block + m * share_y, 8), share_y)
        for half in range(halves):
            part = spectrum[:, half * LANES : (half + 1) * LANES]
            send_f[index % 2, half, :, :, :, rows, :] = part.reshape(
                count // columns, LAYERS, CORES, share_y, LANES
            )

    def send_plane(index, slot, m):
        send_forward(index, 0, slot, m * share_y, share_y, 2 + m)

    def physical(slot, m):
        rows = pl.ds(pl.multiple_of(m * share_y, 8), share_y)
        values = [
            got_i[slot, half, :, :, :, rows, :].reshape(size_y, LANES) for half in range(halves)
        ]
        return mul_right(mul_left(jnp.concatenate(values, axis=1)))

    def spectrum_at(index, half, pair):
        values = [
            got_f[
                index % 2, half, pair // pairs,
                pl.ds(pair % pairs * 2 + inner, size_x, stride=share_y), :,
            ]
            for inner in range(2)
        ]
        return mul_left(jnp.concatenate(values, axis=1))

    def arrived_forward(index, half):
        wait_bytes(got_f.at[index % 2, half, 0], came_f.at[index, half])

        @pl.when(middle)
        def _():
            wait_bytes(
                got_f.at[index % 2, half, :, pl.ds(0, groups * block), :], twin_f.at[index, half]
            )

    def arrived_inverse(index, part):
        rows = pl.ds(pl.multiple_of(part * share_y, 8), share_y)
        wait_bytes(got_i.at[0, :, :, :, :, rows, :], came_i.at[index, part])

        @pl.when(middle)
        def _():
            wait_bytes(got_i.at[:, :, :, 1, :, rows, :], twin_i.at[index, part])

    def inverse(index, sources, update):
        for half in range(halves):
            for source in sources:
                arrived_forward(source, half)
            if index > 0:
                wait_sent(sent_i.at[index - 1, half])

            def step(pair, carry):
                spectra = [spectrum_at(source, half, pair) for source in sources]
                values = mul_left(update(half, pair, *spectra))
                for inner in range(2):
                    send_i[
                        half, pair // pairs,
                        pl.ds(pair % pairs * 2 + inner, size_x, stride=share_y), :,
                    ] = values[:, inner * LANES : (inner + 1) * LANES]
                return carry

            def quarter(number, carry):
                lax.fori_loop(number * units, (number + 1) * units, step, 0)
                if half == 1:
                    pass_inverse(index, 0, number)
                elif index > 0:
                    pass_forward_chunk(sources[-1], number)
                return carry

            lax.fori_loop(0, pairs, quarter, 0)
            if half == 1:
                for source in sources:
                    wait_passed(passed_f.at[source])

            def first_parts(part, carry):
                send_inverse(index, half, part)
                return carry

            lax.fori_loop(0, early, first_parts, 0)

        def last_parts(part, carry):
            for half in range(halves):
                send_inverse(index, half, part)
            return carry

        lax.fori_loop(early, parts, last_parts, 0)
        for part in range(2):
            pass_inverse(index, 1, part)

    def pass_ahead(index, part):
        @pl.when(part + 2 < parts)
        def _():
            pass_inverse(index, 1, part + 2)

        @pl.when(jnp.logical_and(part + 2 >= early, part + 2 < parts))
        def _():
            pass_inverse(index, 0, part + 2)

    def forward(index, stage):
        def step(m, carry):
            pass_ahead(stage, m)
            arrived_inverse(stage, m)

            def one(slot, inner):
                plane(index, slot, m, reaction(physical(slot, m)))
                return inner

            lax.fori_loop(0, units, one, 0)

            @pl.when(m == parts - 1)
            def _():
                wait_passed(passed_i.at[stage])

            def send(slot, inner):
                send_plane(index, slot, m)
                return inner

            lax.fori_loop(0, units, send, 0)

            @pl.when(m >= 2)
            def _():
                pass_forward_part(index, m - 2)

            return carry

        lax.fori_loop(0, parts, step, 0)
        send_second_half(index)
        for part in range(parts - 2, parts):
            pass_forward_part(index, part)

    def wave(indices, length):
        signed = jnp.where(indices * 2 < length, indices, indices - length)
        return wave_scale * signed.astype(jnp.float32) / length

    for m in range(rows_x):
        load(m).start()
    barrier = pltpu.get_barrier_semaphore()

    def greet(offset, carry):
        pl.semaphore_signal(barrier, inc=1, **target((me + offset) % count))
        return carry

    lax.fori_loop(1, count, greet, 0)
    pl.semaphore_wait(barrier, count - 1)

    @pl.when(middle)
    def _():
        for m in range(rows_x):
            swap(m).start()

    def begin_first(m, carry):
        load(m).wait()
        plane(0, home, m, field[home, m])
        send_plane(0, home, m)
        return carry

    def begin_second(m, carry):
        plane(1, home, m, reaction(field[home, m]))
        send_plane(1, home, m)
        return carry

    lax.fori_loop(0, parts, begin_first, 0)
    lax.fori_loop(0, parts, begin_second, 0)

    @pl.when(middle)
    def _():
        other = 1 - home

        def begin_twin(m, carry):
            swap(m).wait_recv()
            plane(0, other, m, field[other, m])
            send_plane(0, other, m)
            plane(1, other, m, reaction(field[other, m]))
            send_plane(1, other, m)
            pass_forward_part(0, m)
            pass_forward_part(1, m)
            return carry

        lax.fori_loop(0, parts, begin_twin, 0)
        for m in range(rows_x):
            swap(m).wait_send()

    for index in range(2):
        send_second_half(index)

    rows_step = 32
    steps = size_x // rows_step

    def factors(item, carry):
        pair = item // steps
        start = pl.multiple_of(item % steps * rows_step, 8)
        where = pl.ds(start, rows_step)
        dims = (rows_step, 2 * LANES)
        lane = lax.broadcasted_iota(jnp.int32, dims, 1)
        second = (lane >= LANES).astype(jnp.int32)
        index_y = second + (unit_at(pair // pairs) * share_y + pair % pairs * 2)
        index_x = lax.broadcasted_iota(jnp.int32, dims, 0) + start
        wave_y, wave_x = wave(index_y, size_y), wave(index_x, size_x)
        for half in range(halves):
            wave_z = wave(lane - second * LANES + half * LANES, size_z)
            ksq = wave_y * wave_y + wave_z * wave_z + wave_x * wave_x
            values = step_factors(ksq)
            for ref, value in zip((e_half, q_half, total, held, f_two, f_three), values):
                ref[half, pair, where, :] = value
        return carry

    lax.fori_loop(0, units * pairs * steps, factors, 0)

    for index in range(2):
        for number in range(chunks):
            pass_forward_chunk(index, number)

    def update_first(half, pair, state_hat, react_u):
        base = e_half[half, pair] * state_hat
        gain = q_half[half, pair] * react_u
        first_hat = base + gain
        total[half, pair] = total[half, pair] * state_hat + held[half, pair] * react_u
        third[half, pair] = e_half[half, pair] * first_hat - gain
        held[half, pair] = base
        return first_hat

    def update_second(half, pair, react_a):
        total[half, pair] = total[half, pair] + 2.0 * f_two[half, pair] * react_a
        return held[half, pair] + q_half[half, pair] * react_a

    def update_third(half, pair, react_b):
        total[half, pair] = total[half, pair] + 2.0 * f_two[half, pair] * react_b
        return third[half, pair] + 2.0 * q_half[half, pair] * react_b

    def update_last(half, pair, react_c):
        return total[half, pair] + f_three[half, pair] * react_c

    inverse(0, (0, 1), update_first)
    for index, update in enumerate((update_second, update_third, update_last)):
        wait_sent_forward(index)
        forward(index + 2, index)
        inverse(index + 1, (index + 2,), update)
    for index in (3, 4):
        wait_sent_forward(index)

    def finish(m, carry):
        pass_ahead(3, m)
        arrived_inverse(3, m)
        field[0, m] = physical(home, m)
        store(m).start()
        return carry

    lax.fori_loop(0, parts, finish, 0)
    wait_passed(passed_i.at[3])
    for half in range(halves):
        wait_sent(sent_i.at[3, half])
    for m in range(rows_x):
        store(m).wait()


def body(initial_field):
    rows_x, size_y, size_z = initial_field.shape
    columns = lax.axis_size("col")
    rows = lax.axis_size("row")
    count = rows * columns
    size_x = rows_x * count
    share_y = size_y // count
    fits = share_y == ROWS and rows_x == ROWS and columns == LAYERS * CORES
    fits = fits and size_z == 2 * LANES and size_x == size_y == size_z
    if not fits:
        return plain_body(initial_field)
    upper, lower = split_table(size_x)
    left = np.concatenate([upper, upper, lower], axis=1)
    right = np.concatenate([upper, upper, lower], axis=0)
    halves, pairs, block = size_z // LANES, share_y // 2, rows_x * share_y
    spectral = pltpu.VMEM((halves, 2 * pairs, size_x, 2 * LANES), jnp.float32)
    vmem = pl.BlockSpec(memory_space=pltpu.VMEM)
    dma = pltpu.SemaphoreType.DMA
    return pl.pallas_call(
        functools.partial(kernel, count, columns, rows_x, share_y, size_x, size_y, size_z),
        out_shape=jax.ShapeDtypeStruct(initial_field.shape, jnp.float32),
        in_specs=[pl.BlockSpec(memory_space=pltpu.HBM), vmem, vmem],
        out_specs=pl.BlockSpec(memory_space=pltpu.HBM),
        scratch_shapes=[
            pltpu.VMEM((2, halves, rows, LAYERS, CORES, 2 * block, LANES), jnp.float32),
            pltpu.VMEM((2, halves, 2, count * block, LANES), jnp.float32),
            pltpu.VMEM((halves, 2, count * block, LANES), jnp.float32),
            pltpu.VMEM((2, halves, rows, LAYERS, CORES, block, LANES), jnp.float32),
        ]
        + [spectral] * 6
        + [
            pltpu.VMEM((2,) + initial_field.shape, jnp.float32),
            dma((5, 2 + rows_x + 4)),
            dma((5, halves)),
            dma((5, halves)),
            dma((5,)),
            dma((4, rows_x)),
            dma((4, halves, rows_x)),
            dma((4, rows_x)),
            dma((4, halves)),
            dma((4,)),
            dma((rows_x,)),
            dma,
            dma((rows_x,)),
            dma((rows_x,)),
        ],
        compiler_params=pltpu.CompilerParams(
            collective_id=0, has_side_effects=True, vmem_limit_bytes=60 * 1024 * 1024
        ),
    )(initial_field, jnp.asarray(left), jnp.asarray(right))


def solution(mesh):
    placed = (P(("row", "col"), None, None),)
    return jax.shard_map(
        body, mesh=mesh, in_specs=placed, out_specs=P(("row", "col"), None, None), check_vma=False
    )
```

time: 419 us -> 397 us (0.947)
  Pallas kernels: 416 us -> 394 us
    pallas_call x1, Pallas kernels: 416 us -> 394 us  [body(): pl.pallas_call(functools.partial(kernel, count, columns, rows_x, share_y,...]
where the time goes in v1:
time: 397 us
  Pallas kernels  394 us (99%)
    pallas_call x1, Pallas kernels, body(): pl.pallas_call(functools.partial(kernel, count, columns, rows_x, share_y,...  394 us

profile of v1, /device:TPU:0, one launch (start us, length us, event | category | flops | bytes accessed | tf_op | source)
XLA Modules:
  0.0 397.1 jit_solution(1990918267327888058)
XLA Ops:
  0.0 394.0 %shard_map.37 = f32[8,256,256]{2,1,0:T(8,128)} custom-call(f32[8,256,256]{2,1,0:T(8,128)} %field_in.1, bf16[256,768]{1,0:T(8,128)(2,1)} %constant.4.clone.left, bf16[768,256]{1,0:T(8,128)(2,1)} %constant.5.clone.right), custom_call_target="tpu_custom_call" | custom-call | tf_op jit(solution)/shard_map/pallas_call | solution.py:687
  394.0 3.0 copy.5
